TPU v7x, 256 devices: a whole 4x4x8 slice. The times are simulated.
256 devices in a mesh: expert: 16 (over x, y), tensor: 8 (over z), replica: 2 (over core).
Axes of the slice: x: 4, y: 4, z: 8, core: 2. Of those that a mesh axis runs over, the one named last changes fastest.
Arguments:
- trained: float32 [16, 7168, 2048], P('replica', 'tensor', 'expert'), may hold values from -3080 to 3080
- snapshot: bfloat16 [16, 7168, 2048], P('replica', 'tensor', 'expert'), may hold values from -3072 to 3072
- changed: int32 [16, 56, 16], P('replica', 'tensor', 'expert'), may hold values from 0 to 1, as said below
- placement: int32 [16], replicated, may hold values from 0 to 15, each once
Outputs:
- rotated_update: bfloat16 [16, 7168, 2048], P('expert', None, 'tensor')
Inputs may be any that keep to these rules, and one draw needn't show every extreme that they name: `placement`: each of the 16 experts appears exactly once. `changed`: in each aligned block of 7 block rows by 1 block columns of one expert, at most 4 entries are 1; for every expert some such block has exactly 4.
All inputs are finite; a program needn't handle non-finite values.
Results may differ from a plain program's by a relative error of at most 0.001.
Values may be sent and summed in bfloat16 or wider, within the bound.
A program may use at most 64 MiB of HBM per device.

v0:
```python
import math

import jax
import jax.numpy as jnp
from jax import lax
from jax.sharding import PartitionSpec as P

BLK = 128


def hadamard():
    positions = jnp.arange(BLK, dtype=jnp.int32)
    parity = jnp.zeros((BLK, BLK), jnp.int32)
    for bit_level in range(BLK.bit_length() - 1):
        parity = parity + (positions[:, None] >> bit_level & 1) * (
            positions[None, :] >> bit_level & 1
        )
    return (1 - 2 * (parity % 2)).astype(jnp.float32) / math.sqrt(BLK)


def body(trained, snapshot, changed, placement):
    hadamard_table = hadamard()
    local_experts, local_rows, local_cols = trained.shape
    copies = lax.axis_size("replica")
    tensor_count = lax.axis_size("tensor")
    expert_count = lax.axis_size("expert")
    members = expert_count // tensor_count
    slot_total = placement.shape[0]
    owner_slots = slot_total // expert_count
    block_rows = local_rows // BLK
    block_cols = local_cols // BLK
    part_rows = BLK // copies
    block_count = block_rows * block_cols
    capacity = (4 * block_count + 3) // 7
    block_flags = changed.reshape(local_experts, block_count)
    position = jnp.arange(block_count, dtype=jnp.int32)
    ranking = jnp.where(block_flags == 1, position[None, :], block_count + position[None, :])
    picked = jnp.argsort(ranking, axis=1)[:, :capacity]
    used_slots = jnp.take_along_axis(block_flags, picked, axis=1)
    expert_ids = jnp.arange(local_experts, dtype=jnp.int32)[:, None]
    row_ids = picked // block_cols
    col_ids = picked % block_cols
    new_tiles = trained.reshape(local_experts, block_rows, BLK, block_cols, BLK)[
        expert_ids, row_ids, :, col_ids, :
    ]
    old_tiles = snapshot.reshape(local_experts, block_rows, BLK, block_cols, BLK)[
        expert_ids, row_ids, :, col_ids, :
    ]
    delta_tiles = jnp.where(
        used_slots[:, :, None, None] == 1, new_tiles - old_tiles.astype(jnp.float32), 0.0
    )
    coded_tiles = jnp.einsum(
        "ij,pmjk->pmik", hadamard_table, delta_tiles, precision=lax.Precision.HIGHEST
    ).astype(jnp.bfloat16)
    coded_tiles = coded_tiles.reshape(local_experts, capacity, copies, part_rows, BLK)
    spots_pair = jnp.broadcast_to(picked[:, :, None], (local_experts, capacity, copies))
    tiles_all, spots_all = (
        lax.all_to_all(coded_tiles, "replica", split_axis=2, concat_axis=0, tiled=True),
        lax.all_to_all(spots_pair, "replica", split_axis=2, concat_axis=0, tiled=True),
    )
    chosen = jnp.take(tiles_all, placement, axis=0).reshape(
        slot_total, 1, 1, capacity, part_rows, BLK
    )
    chosen_spots = jnp.take(spots_all, placement, axis=0).reshape(slot_total, 1, 1, capacity)
    tiles_in, spot_numbers = (
        lax.all_to_all(
            lax.all_to_all(chosen, "expert", split_axis=0, concat_axis=2, tiled=True),
            "tensor",
            split_axis=2,
            concat_axis=1,
            tiled=True,
        ),
        lax.all_to_all(
            lax.all_to_all(chosen_spots, "expert", split_axis=0, concat_axis=2, tiled=True),
            "tensor",
            split_axis=2,
            concat_axis=1,
            tiled=True,
        ),
    )
    source_count = tiles_in.shape[1]
    one_hot = (spot_numbers[..., None] == position).astype(jnp.bfloat16)
    placed = jnp.einsum(
        "osnmg,osnmab->osngab", one_hot, tiles_in, preferred_element_type=jnp.float32
    ).astype(jnp.bfloat16)
    placed = placed.reshape(
        owner_slots, source_count, members, block_rows, block_cols, part_rows, BLK
    )
    placed = jnp.transpose(placed, (0, 1, 3, 5, 2, 4, 6))
    owner_cols = members * block_cols * BLK
    owned_rows = placed.reshape(owner_slots, source_count, block_rows, 1, part_rows, owner_cols)
    whole_rows = lax.all_gather(owned_rows, "replica", axis=3, tiled=True)
    return whole_rows.reshape(owner_slots, tensor_count * block_rows * BLK, owner_cols)


def solution(mesh):
    in_specs = (
        P("replica", "tensor", "expert"),
        P("replica", "tensor", "expert"),
        P("replica", "tensor", "expert"),
        P(),
    )
    out_specs = P("expert", None, "tensor")
    return jax.shard_map(body, mesh=mesh, in_specs=in_specs, out_specs=out_specs, check_vma=False)
```

profile of v0, /device:TPU:33, one launch (start us, length us, event | category | flops | bytes accessed | tf_op | source)
XLA Modules:
  0.0 143.7 jit_solution(11660733728816668597)
XLA Ops:
  6.5 0.0 copy-start
  6.5 0.9 iota_select_fusion
  7.4 0.7 sort.17
  8.1 0.6 broadcast_in_dim.55
  8.7 3.9 %all-to-all-start = ((s32[8,4,2]{0,1,2:T(4,128)}), s32[8,4,2]{0,1,2:T(4,128)S(1)}, u32[]{:S(2)}, u32[]{:S(2)}) async-start(s32[8,4,2]{0,1,2:T(4,128)} %broadcast_in_dim.55), calls=%async_computation | async-start | bytes 8192 | tf_op jit(solution)/shard_map/all_to_all | solution.py:59
  12.6 0.7 compare_and_fusion
  13.2 0.7 compare_select_fusion.1
  13.9 0.8 copy.38
  14.7 0.1 copy.46
  14.8 0.1 reshape.261
  14.9 0.7 gather_fusion.4
  15.5 0.1 reshape.264
  15.6 0.1 copy.47
  15.7 0.1 copy.48
  15.8 0.0 copy-done
  15.8 0.8 gather_fusion.2
  16.6 4.0 %gather_fusion.1 = f32[32,128,128]{2,1,0:T(8,128)} fusion(f32[8,7,128,1,128]{4,2,1,0,3:T(8,128)} %bitcast.67, s32[32]{0:T(128)S(1)} %reshape.261), kind=kCustom, calls=%fused_computation.1 | custom fusion | bytes 4194688 | tf_op jit(solution)/shard_map/gather | solution.py:43
  20.6 1.9 %convert_subtract_fusion = f32[32,128,128]{2,1,0:T(8,128)S(1)} fusion(f32[32,128,128]{2,1,0:T(8,128)} %gather_fusion.1, bf16[32,128,128]{2,1,0:T(8,128)(2,1)S(1)} %gather_fusion.2), kind=kLoop, calls=%fused_computation.5 | loop fusion | flops 1048576 | bytes 5242880 | tf_op jit(solution)/shard_map/sub | solution.py:50
  22.5 2.3 %fusion.2 = bf16[8,4,128,128]{2,3,1,0:T(8,128)(2,1)S(1)} fusion(f32[8,4,128,128]{3,2,1,0:T(8,128)S(1)} %bitcast.61, pred[8,4]{1,0:T(8,128)(4,1)S(1)} %copy.48, s32[128]{0:T(128)S(1)} %get-tuple-element.7, s32[128]{0:T(128)S(1)} %get-tuple-element.8, s32[128]{0:T(128)S(1)} %get-tuple-element.9, s32[128]{0:T(128)S(1)} %get-tuple-element.10, ...), kind=kOutput, calls=%fused_computation.9 | convolution fusion | flops 806813696 | bytes 3149344 | tf_op jit(solution)/shard_map/ij,pmjk->pmik/dot_general | solution.py:52
  24.8 1.1 copy.49
  25.9 0.0 all-to-all-done
  25.9 3.6 %all-to-all-start.3 = ((bf16[8,4,2,64,128]{4,3,1,0,2:T(8,128)(2,1)}), bf16[8,4,2,64,128]{4,3,1,0,2:T(8,128)(2,1)S(1)}, u32[]{:S(2)}, u32[]{:S(2)}) async-start(bf16[8,4,2,64,128]{4,3,1,0,2:T(8,128)(2,1)} %copy.49), calls=%async_computation.3 | async-start | bytes 2097152 | tf_op jit(solution)/shard_map/all_to_all | solution.py:58
  29.5 0.1 copy.59
  29.6 0.6 gather_fusion
  30.1 0.1 copy.42
  30.2 0.7 copy.43
  30.9 0.3 all-to-all-done.3
  31.2 0.0 copy-start.1
  31.2 6.8 %all-to-all-start.1 = ((s32[16,1,1,4]{3,2,1,0:T(1,128)}), s32[16,1,1,4]{3,2,1,0:T(1,128)}, u32[]{:S(2)}, u32[]{:S(2)}) async-start(s32[16,1,1,4]{3,2,1,0:T(1,128)} %copy.43), calls=%async_computation.1 | async-start | bytes 16384 | tf_op jit(solution)/shard_map/all_to_all | solution.py:74
  38.0 0.0 copy-done.1
  38.0 2.0 %gather_fusion.3 = bf16[16,4,64,128]{3,2,1,0:T(8,128)(2,1)S(1)} fusion(bf16[16,4,64,128]{3,2,1,0:T(8,128)(2,1)} %bitcast.65, s32[1024]{0:T(1024)S(1)} %pad_clamp_fusion), kind=kCustom, calls=%fused_computation.3 | custom fusion | bytes 2097216 | tf_op jit(solution)/shard_map/jit(_take)/gather | solution.py:61
  40.0 1.1 fusion.5
  41.2 3.2 %all-to-all-done.1 = s32[16,1,1,4]{3,2,1,0:T(1,128)} async-done(((s32[16,1,1,4]{3,2,1,0:T(1,128)}), s32[16,1,1,4]{3,2,1,0:T(1,128)}, u32[]{:S(2)}, u32[]{:S(2)}) %all-to-all-start.1) | async-done | bytes 288 | tf_op jit(solution)/shard_map/all_to_all | solution.py:74
  44.4 18.6 %all_to_all.78 = bf16[16,1,1,4,64,128]{5,4,3,2,1,0:T(8,128)(2,1)S(1)} all-to-all(bf16[16,1,1,4,64,128]{5,4,3,2,1,0:T(8,128)(2,1)} %fusion.5), channel_id=1, replica_groups=mesh['expert'=16,'tensor'=8,'replica'=2] {'expert'}, dimensions={0} | all-to-all | bytes 2097152 | tf_op jit(solution)/shard_map/all_to_all | solution.py:67
  62.9 30.6 %all_to_all.79 = bf16[1,1,16,4,64,128]{5,4,3,1,0,2:T(8,128)(2,1)} all-to-all(bf16[1,1,16,4,64,128]{5,4,3,1,0,2:T(8,128)(2,1)S(1)} %bitcast.66), channel_id=1, replica_groups=mesh['expert'=16,'tensor'=8,'replica'=2] {'tensor'}, dimensions={2} | all-to-all | bytes 2097152 | tf_op jit(solution)/shard_map/all_to_all | solution.py:66
  93.6 6.0 %all-to-all-start.2 = ((s32[1,1,16,4]{3,1,0,2:T(1,128)}), s32[1,1,16,4]{3,1,0,2:T(1,128)S(1)}, u32[]{:S(2)}, u32[]{:S(2)}) async-start(s32[1,1,16,4]{3,1,0,2:T(1,128)} %bitcast.31), calls=%async_computation.2 | async-start | bytes 16384 | tf_op jit(solution)/shard_map/all_to_all | solution.py:73
  99.6 0.0 all-gather.2.cloned.1.call-start
  99.6 2.1 %copy.52 = bf16[1,1,16,4,64,128]{5,3,4,2,1,0:T(4,128)(2,1)S(1)} copy(bf16[1,1,16,4,64,128]{5,4,3,1,0,2:T(8,128)(2,1)} %all_to_all.79) | data formatting | bytes 2097152 | tf_op jit(solution)/shard_map/all_to_all | solution.py:66
  101.7 3.3 %all-to-all-done.2 = s32[1,1,16,4]{3,1,0,2:T(1,128)S(1)} async-done(((s32[1,1,16,4]{3,1,0,2:T(1,128)}), s32[1,1,16,4]{3,1,0,2:T(1,128)S(1)}, u32[]{:S(2)}, u32[]{:S(2)}) %all-to-all-start.2) | async-done | bytes 288 | tf_op jit(solution)/shard_map/all_to_all | solution.py:73
  105.0 1.3 convert_bitcast_fusion
  106.4 3.3 %copy.53 = bf16[1,8,7,64,2,1,128]{6,4,3,2,1,5,0:T(2,128)(2,1)} copy(bf16[1,8,7,64,2,1,128]{6,2,3,4,1,5,0:T(8,128)(2,1)S(1)} %convert_bitcast_fusion) | data formatting | bytes 3670016 | tf_op jit(solution)/shard_map/transpose | solution.py:89
  109.6 5.3 %reshape.227 = bf16[1,8,7,1,64,256]{5,4,2,1,3,0:T(8,128)(2,1)} reshape(bf16[1,8,7,64,2,1,128]{6,4,3,2,1,5,0:T(2,128)(2,1)} %copy.53) | data formatting | bytes 3670016 | tf_op jit(solution)/shard_map/reshape | solution.py:91
  114.9 0.0 all-gather.2.cloned.1.call-update
  115.0 17.5 %all-gather.2.cloned.1.call-done = bf16[1,8,7,2,64,256]{5,4,2,1,0,3:T(8,128)(2,1)} async-done(((bf16[1,8,7,1,64,256]{5,4,2,1,0,3:T(8,128)(2,1)}), bf16[1,8,7,2,64,256]{5,4,2,1,0,3:T(8,128)(2,1)}) %all-gather.2.cloned.1.call-update) | async-done | bytes 3670032 | tf_op jit(solution)/shard_map/all_gather | solution.py:92
  132.5 4.4 %copy.55 = bf16[1,8,7,2,64,256]{5,4,3,2,1,0:T(8,128)(2,1)} copy(bf16[1,8,7,2,64,256]{5,4,2,1,0,3:T(8,128)(2,1)} %all-gather.2.cloned.1.call-done) | data formatting | bytes 7340032 | tf_op jit(solution)/shard_map/all_gather | solution.py:92
  (11 shorter events, 0.1 us)
Async XLA Ops:
  6.5 9.3 %copy-start = (bf16[8,896,128]{2,1,0:T(8,128)(2,1)S(1)}, bf16[8,896,128]{2,1,0:T(8,128)(2,1)}, u32[]{:S(2)}) copy-start(bf16[8,896,128]{2,1,0:T(8,128)(2,1)} %param.5) | copy-start | bytes 5505028
  8.7 17.2 %all-to-all-start = ((s32[8,4,2]{0,1,2:T(4,128)}), s32[8,4,2]{0,1,2:T(4,128)S(1)}, u32[]{:S(2)}, u32[]{:S(2)}) async-start(s32[8,4,2]{0,1,2:T(4,128)} %broadcast_in_dim.55), calls=%async_computation | async-start | bytes 8192 | tf_op jit(solution)/shard_map/all_to_all | solution.py:59
  25.9 5.3 %all-to-all-start.3 = ((bf16[8,4,2,64,128]{4,3,1,0,2:T(8,128)(2,1)}), bf16[8,4,2,64,128]{4,3,1,0,2:T(8,128)(2,1)S(1)}, u32[]{:S(2)}, u32[]{:S(2)}) async-start(bf16[8,4,2,64,128]{4,3,1,0,2:T(8,128)(2,1)} %copy.49), calls=%async_computation.3 | async-start | bytes 2097152 | tf_op jit(solution)/shard_map/all_to_all | solution.py:58
  31.2 6.8 %copy-start.1 = (bf16[8,4,2,64,128]{4,3,1,0,2:T(8,128)(2,1)}, bf16[8,4,2,64,128]{4,3,1,0,2:T(8,128)(2,1)S(1)}, u32[]{:S(2)}) copy-start(bf16[8,4,2,64,128]{4,3,1,0,2:T(8,128)(2,1)S(1)} %all-to-all-done.3) | copy-start | bytes 3145732
  31.2 13.1 %all-to-all-start.1 = ((s32[16,1,1,4]{3,2,1,0:T(1,128)}), s32[16,1,1,4]{3,2,1,0:T(1,128)}, u32[]{:S(2)}, u32[]{:S(2)}) async-start(s32[16,1,1,4]{3,2,1,0:T(1,128)} %copy.43), calls=%async_computation.1 | async-start | bytes 16384 | tf_op jit(solution)/shard_map/all_to_all | solution.py:74
  93.6 11.5 %all-to-all-start.2 = ((s32[1,1,16,4]{3,1,0,2:T(1,128)}), s32[1,1,16,4]{3,1,0,2:T(1,128)S(1)}, u32[]{:S(2)}, u32[]{:S(2)}) async-start(s32[1,1,16,4]{3,1,0,2:T(1,128)} %bitcast.31), calls=%async_computation.2 | async-start | bytes 16384 | tf_op jit(solution)/shard_map/all_to_all | solution.py:73
  99.6 32.8 %all-gather.2.cloned.1.call-start = ((), (), s32[]{:S(2)}) async-start(), calls=%async_computation.6 | async-start | bytes 5505024 | tf_op jit(solution)/shard_map/all_gather | solution.py:92
Sparse Core Ops, SparseCore 0:
  115.1 17.3 all-gather.1
where the time goes:
time: 146 us; the launch traced here: 144 us
  blocking collectives  49.2 us (34%)
  local copies, waits for them, and re-layouts  26.8 us (18%)
  waiting for transfers between devices  24.4 us (17%)
  starting transfers between devices  20.3 us (14%)
  between operations  13.5 us (9%)
  other arithmetic  5.93 us (4%)
  matrix products  3.58 us (2%)
    all_to_all x1, blocking collectives, body(): lax.all_to_all(lax.all_to_all(chosen, 'expert', split_axis=0, concat_axis...  30.6 us
    all_to_all x1, blocking collectives, body(): lax.all_to_all(chosen, 'expert', split_axis=0, concat_axis=2, tiled=True)  18.6 us
    all_gather x1, waiting for transfers between devices, body(): whole_rows = lax.all_gather(owned_rows, 'replica', axis=3, tiled=True)  17.5 us
    all_to_all x1, starting transfers between devices, body(): lax.all_to_all(chosen_spots, 'expert', split_axis=0, concat_axis=2, tiled...  6.8 us
    all_to_all x1, starting transfers between devices, body(): lax.all_to_all(lax.all_to_all(chosen_spots, 'expert', split_axis=0, conca...  6.05 us
    reshape x1, local copies, waits for them, and re-layouts, body(): placed.reshape(owner_slots, source_count, block_rows, 1, part_rows, owner...  5.3 us
    all_gather x1, local copies, waits for them, and re-layouts, body(): whole_rows = lax.all_gather(owned_rows, 'replica', axis=3, tiled=True)  4.37 us
    gather x1, local copies, waits for them, and re-layouts, body(): trained.reshape(local_experts, block_rows, BLK, block_cols, BLK)  4.04 us
  transfers between devices with their start and end apart: 5, of which 4 were waited for; matrix products, arithmetic and copies ran while one was open for 14% of the time, Pallas kernels for 0%

commit v1 on v0

v1 whole, which is shorter than its diff:
```python
import math

import jax
import jax.numpy as jnp
from jax import lax
from jax.experimental import pallas as pl
from jax.experimental.pallas import tpu as pltpu
from jax.sharding import PartitionSpec as P

MESH = pl.DeviceIdType.MESH
BLK = 128
MOST = 4
HALF = MOST // 2
META = 16
ROWS = HALF * BLK + META


def sign_table(rows, cols):
    shared = lax.broadcasted_iota(jnp.int32, (rows, cols), 0) & (
        lax.broadcasted_iota(jnp.int32, (rows, cols), 1) & (BLK - 1)
    )
    shared = shared ^ (shared >> 4)
    shared = shared ^ (shared >> 2)
    shared = shared ^ (shared >> 1)
    return (1 - 2 * (shared & 1)).astype(jnp.float32).astype(jnp.bfloat16)


def push_kernel(sizes, trained, snapshot, changed, placement, result, new_bufs, old_bufs, table, mine, other, staged, passing, sems):
    expert_count, tensor_count, local_experts, block_rows = sizes
    (in_sem, swap_send, swap_recv, plane_send, plane_recv, z_send, z_recv, last_send, last_recv) = sems
    c = lax.axis_index("expert")
    z = lax.axis_index("tensor")
    r = lax.axis_index("replica")
    slots = expert_count
    group = expert_count // tensor_count

    barrier = pltpu.get_barrier_semaphore()

    pl.semaphore_signal(barrier, inc=1, device_id=(c, z, 1 - r), device_id_type=MESH)

    @pl.loop(1, expert_count)
    def _(step):
        pl.semaphore_signal(barrier, inc=1, device_id=(lax.rem(c + step, expert_count), z, r), device_id_type=MESH)

    @pl.loop(1, tensor_count)
    def _(step):
        pl.semaphore_signal(barrier, inc=1, device_id=(c, lax.rem(z + step, tensor_count), r), device_id_type=MESH)

    def loads(e):
        return (
            pltpu.make_async_copy(trained.at[e], new_bufs[e], in_sem.at[0, e]),
            pltpu.make_async_copy(snapshot.at[e], old_bufs[e], in_sem.at[1, e]),
        )

    for e in range(local_experts):
        for load in loads(e):
            load.start()

    table[...] = sign_table(BLK, 2 * BLK)
    pl.semaphore_wait(barrier, expert_count + tensor_count - 1)

    def swap(e):
        return pltpu.make_async_remote_copy(
            src_ref=other.at[e],
            dst_ref=mine.at[r * local_experts + e],
            send_sem=swap_send.at[e],
            recv_sem=swap_recv.at[e],
            device_id=(c, z, 1 - r),
            device_id_type=MESH,
        )

    row_ids = lax.broadcasted_iota(jnp.int32, (META, BLK), 0)

    for e in range(local_experts):
        for load in loads(e):
            load.wait()
        count = jnp.int32(0)
        spots = [jnp.int32(block_rows)] * MOST
        picks = [jnp.int32(0)] * MOST
        for b in range(block_rows):
            flag = changed[e, b]
            for k in range(MOST):
                hit = (flag == 1) & (count == k)
                spots[k] = jnp.where(hit, b, spots[k])
                picks[k] = jnp.where(hit, b, picks[k])
            count = count + flag
        highs, lows = [], []
        for k in range(MOST):
            delta = new_bufs[e][picks[k]] - old_bufs[e][picks[k]].astype(jnp.float32)
            high = delta.astype(jnp.bfloat16)
            highs.append(high)
            lows.append((delta - high.astype(jnp.float32)).astype(jnp.bfloat16))
        parts = jnp.concatenate([jnp.concatenate(highs, axis=1), jnp.concatenate(lows, axis=1)], axis=0)
        coded = jnp.dot(table[...], parts, preferred_element_type=jnp.float32) * (1.0 / math.sqrt(BLK))
        coded = coded.astype(jnp.bfloat16)

        def store(ref, index, first, coded=coded, spots=spots):
            for k in range(HALF):
                ref[index, k * BLK : (k + 1) * BLK, :] = coded[:, (first + k) * BLK : (first + k + 1) * BLK]
            spot = jnp.where(row_ids < META // 2, spots[first], spots[first + 1])
            ref[index, HALF * BLK : ROWS, :] = spot.astype(jnp.float32).astype(jnp.bfloat16)

        own = r * local_experts + e

        @pl.when(r == 0)
        def _():
            store(mine, own, 0)
            store(other, e, HALF)

        @pl.when(r == 1)
        def _():
            store(mine, own, HALF)
            store(other, e, 0)

        if e > 0:
            swap(e - 1).start()

    swap(local_experts - 1).start()

    @pl.loop(0, local_experts)
    def _(e):
        swap(e).wait_recv()

    home = c // group == z

    @pl.when(home)
    def _():
        result[r, c] = mine[placement[c]]

    @pl.when(jnp.logical_not(home))
    def _():
        passing[c] = mine[placement[c]]

    spot_here = z * group + lax.rem(c, group)

    def plane(s):
        return pltpu.make_async_remote_copy(
            src_ref=staged.at[s],
            dst_ref=passing.at[c],
            send_sem=plane_send.at[s],
            recv_sem=plane_recv.at[c],
            device_id=(s, z, r),
            device_id_type=MESH,
        )

    def plane_home(s):
        return pltpu.make_async_remote_copy(
            src_ref=staged.at[s],
            dst_ref=result.at[r, spot_here],
            send_sem=plane_send.at[s],
            recv_sem=z_recv.at[spot_here],
            device_id=(s, z, r),
            device_id_type=MESH,
        )

    def shift(step):
        turn = lax.rem(step, 2) * (slots // 2) + step // 2
        return lax.rem(turn + group * z, slots)

    @pl.loop(0, slots)
    def _(step):
        s = lax.rem(c + slots - shift(step), slots)

        @pl.when(s != c)
        def _():
            staged[s] = mine[placement[s]]

            @pl.when(home)
            def _():
                plane_home(s).start()

            @pl.when(jnp.logical_not(home))
            def _():
                plane(s).start()

    def along(source):
        spot = z * group + lax.rem(source, group)
        return pltpu.make_async_remote_copy(
            src_ref=passing.at[source],
            dst_ref=result.at[r, spot],
            send_sem=z_send.at[source],
            recv_sem=z_recv.at[spot],
            device_id=(c, source // group, r),
            device_id_type=MESH,
        )

    def plane_from(source):
        return pltpu.make_async_remote_copy(
            src_ref=staged.at[source],
            dst_ref=passing.at[source],
            send_sem=plane_send.at[source],
            recv_sem=plane_recv.at[source],
            device_id=(source, z, r),
            device_id_type=MESH,
        )

    @pl.loop(0, slots)
    def _(step):
        source = lax.rem(c + shift(step), slots)

        @pl.when(source // group != z)
        def _():
            @pl.when(source != c)
            def _():
                plane_from(source).wait_recv()

            along(source).start()

    def last(spot):
        return pltpu.make_async_remote_copy(
            src_ref=result.at[r, spot],
            dst_ref=result.at[r, spot],
            send_sem=last_send.at[spot],
            recv_sem=last_recv.at[spot],
            device_id=(c, z, 1 - r),
            device_id_type=MESH,
        )

    def arrived(spot):
        return pltpu.make_async_remote_copy(
            src_ref=result.at[r, spot],
            dst_ref=result.at[r, spot],
            send_sem=z_send.at[spot],
            recv_sem=z_recv.at[spot],
            device_id=(c, z, 1 - r),
            device_id_type=MESH,
        )

    def last_from(spot):
        return pltpu.make_async_remote_copy(
            src_ref=result.at[1 - r, spot],
            dst_ref=result.at[1 - r, spot],
            send_sem=last_send.at[spot],
            recv_sem=last_recv.at[spot],
            device_id=(c, z, 1 - r),
            device_id_type=MESH,
        )

    @pl.loop(0, slots)
    def _(step):
        turn = lax.rem(step, 2) * (slots // 2) + step // 2
        spot = lax.rem(z * group + slots - turn, slots)

        @pl.when(jnp.logical_not(home & (spot == c)))
        def _():
            arrived(spot).wait_recv()

        last(spot).start()

    @pl.loop(0, local_experts)
    def _(e):
        swap(e).wait_send()

    @pl.loop(0, slots)
    def _(s):
        @pl.when(s != c)
        def _():
            plane(s).wait_send()

        @pl.when(s // group != z)
        def _():
            along(s).wait_send()

        last(s).wait_send()
        last_from(s).wait_recv()


def push(trained, snapshot, changed, placement):
    local_experts, block_rows = changed.shape
    slots = placement.shape[0]
    sizes = (lax.axis_size("expert"), lax.axis_size("tensor"), local_experts, block_rows)
    dma = pltpu.SemaphoreType.DMA

    def kernel(a, b, c, d, result, *refs):
        new_bufs, old_bufs, refs = refs[:local_experts], refs[local_experts : 2 * local_experts], refs[2 * local_experts :]
        push_kernel(sizes, a, b, c, d, result, new_bufs, old_bufs, *refs[:5], refs[5:])

    return pl.pallas_call(
        kernel,
        name="push",
        out_shape=jax.ShapeDtypeStruct((2, slots, ROWS, BLK), jnp.bfloat16),
        in_specs=[
            pl.BlockSpec(memory_space=pltpu.HBM),
            pl.BlockSpec(memory_space=pltpu.HBM),
            pl.BlockSpec(memory_space=pltpu.SMEM),
            pl.BlockSpec(memory_space=pltpu.SMEM),
        ],
        out_specs=pl.BlockSpec(memory_space=pltpu.VMEM),
        scratch_shapes=[
            *[pltpu.VMEM(trained.shape[1:], jnp.float32) for _ in range(local_experts)],
            *[pltpu.VMEM(snapshot.shape[1:], jnp.bfloat16) for _ in range(local_experts)],
            pltpu.VMEM((BLK, 2 * BLK), jnp.bfloat16),
            pltpu.VMEM((slots, ROWS, BLK), jnp.bfloat16),
            pltpu.VMEM((local_experts, ROWS, BLK), jnp.bfloat16),
            pltpu.VMEM((slots, ROWS, BLK), jnp.bfloat16),
            pltpu.VMEM((slots, ROWS, BLK), jnp.bfloat16),
            dma((2, local_experts)),
            dma((local_experts,)),
            dma((local_experts,)),
            dma((slots,)),
            dma((slots,)),
            dma((slots,)),
            dma((slots,)),
            dma((slots,)),
            dma((slots,)),
        ],
        compiler_params=pltpu.CompilerParams(collective_id=0, has_side_effects=True, vmem_limit_bytes=60 * 1024 * 1024),
    )(trained, snapshot, changed, placement)


def spread_kernel(sizes, tiles, out, image, sems):
    tensor_count, group, block_rows = sizes

    def write(z):
        rows = pl.ds(pl.multiple_of(z * block_rows * BLK, BLK), block_rows * BLK)
        return pltpu.make_async_copy(image.at[z], out.at[0, rows, :], sems.at[z])

    @pl.loop(0, tensor_count)
    def _(z):
        for j in range(group):
            index = z * group + j
            spots = []
            for k in range(MOST):
                row = HALF * BLK + (k % HALF) * (META // HALF)
                spots.append(tiles[k // HALF, index, row : row + 1, :])
            chunk = 32
            for b in range(block_rows):
                masks = [jnp.broadcast_to(spots[k] == jnp.bfloat16(b), (chunk, BLK)) for k in range(MOST)]
                for first in range(0, BLK, chunk):
                    value = jnp.zeros((chunk, BLK), jnp.bfloat16)
                    for k in range(MOST):
                        row = (k % HALF) * BLK + first
                        value = jnp.where(masks[k], tiles[k // HALF, index, row : row + chunk, :], value)
                    image[z, b * BLK + first : b * BLK + first + chunk, j * BLK : (j + 1) * BLK] = value
        write(z).start()

    @pl.loop(0, tensor_count)
    def _(z):
        write(z).wait()


def spread(tiles, block_rows):
    tensor_count = lax.axis_size("tensor")
    group = tiles.shape[1] // tensor_count
    rows = block_rows * BLK

    def kernel(tiles_ref, out, image, sems):
        spread_kernel((tensor_count, group, block_rows), tiles_ref, out, image, sems)

    return pl.pallas_call(
        kernel,
        name="spread",
        out_shape=jax.ShapeDtypeStruct((1, tensor_count * rows, group * BLK), jnp.bfloat16),
        in_specs=[pl.BlockSpec(memory_space=pltpu.VMEM)],
        out_specs=pl.BlockSpec(memory_space=pl.ANY),
        scratch_shapes=[
            pltpu.VMEM((tensor_count, rows, group * BLK), jnp.bfloat16),
            pltpu.SemaphoreType.DMA((tensor_count,)),
        ],
        compiler_params=pltpu.CompilerParams(vmem_limit_bytes=24 * 1024 * 1024),
    )(tiles)


def body(trained, snapshot, changed, placement):
    local_experts, local_rows, _ = trained.shape
    block_rows = local_rows // BLK
    blocks = (local_experts, block_rows, BLK, BLK)
    tiles = push(trained.reshape(blocks), snapshot.reshape(blocks), changed.reshape(local_experts, block_rows), placement)
    return spread(tiles, block_rows)


def solution(mesh):
    in_specs = (
        P("replica", "tensor", "expert"),
        P("replica", "tensor", "expert"),
        P("replica", "tensor", "expert"),
        P(),
    )
    out_specs = P("expert", None, "tensor")
    return jax.shard_map(body, mesh=mesh, in_specs=in_specs, out_specs=out_specs, check_vma=False)
```

time: 146 us -> 58.9 us (0.40)
  the two profiles are of different devices: /device:TPU:33 before, /device:TPU:1 now
where the time goes in v1:
time: 58.9 us; the launch traced here: 58.7 us
  Pallas kernels  55.7 us (95%)
  local copies, waits for them, and re-layouts  2.97 us (5%)
    pallas_call x1, Pallas kernels, push(): pl.pallas_call(kernel, name='push', out_shape=jax.ShapeDtypeStruct((2, sl...  53.1 us
    unnamed x3, local copies, waits for them, and re-layouts  2.97 us
    pallas_call x1, Pallas kernels, spread(): pl.pallas_call(kernel, name='spread', out_shape=jax.ShapeDtypeStruct((1,...  2.62 us

profile of v1, /device:TPU:1, one launch (start us, length us, event | category | flops | bytes accessed | tf_op | source)
XLA Modules:
  0.0 58.7 jit_solution(5784513327269129783)
XLA Ops:
  0.0 1.4 %copy.5 = s32[8,7,1]{1,0,2:T(8,128)} copy(s32[8,7,1]{0,2,1:T(1,128)} %param.6) | data formatting | bytes 448 | tf_op args[2]
  1.4 53.1 %push.1.tiles_ref = bf16[2,16,272,128]{3,2,1,0:T(8,128)(2,1)} custom-call(f32[8,7,128,128]{3,2,1,0:T(8,128)} %bitcast.3, bf16[8,7,128,128]{3,2,1,0:T(8,128)(2,1)} %bitcast.4, s32[8,7]{1,0:T(8,128)} %bitcast.5, s32[16]{0:T(128)} %d.1), custom_call_target="tpu_custom_call" | custom-call | tf_op jit(solution)/shard_map/push/pallas_call | solution.py:278
  54.5 0.0 copy-start
  54.5 1.6 %copy-done = bf16[2,16,272,128]{3,2,1,0:T(8,128)(2,1)S(1)} copy-done((bf16[2,16,272,128]{3,2,1,0:T(8,128)(2,1)S(1)}, bf16[2,16,272,128]{3,2,1,0:T(8,128)(2,1)}, u32[]{:S(2)}) %copy-start) | copy-done | bytes 2228248
  56.1 2.6 %spread.1 = bf16[1,7168,256]{2,1,0:T(8,128)(2,1)} custom-call(bf16[2,16,272,128]{3,2,1,0:T(8,128)(2,1)S(1)} %copy-done), custom_call_target="tpu_custom_call" | custom-call | tf_op jit(solution)/shard_map/spread/pallas_call | solution.py:350
Async XLA Ops:
  54.5 1.6 %copy-start = (bf16[2,16,272,128]{3,2,1,0:T(8,128)(2,1)S(1)}, bf16[2,16,272,128]{3,2,1,0:T(8,128)(2,1)}, u32[]{:S(2)}) copy-start(bf16[2,16,272,128]{3,2,1,0:T(8,128)(2,1)} %push.1.tiles_ref) | copy-start | bytes 6684676

commit v2 on v1

v2 whole, which is shorter than its diff:
```python
import math

import jax
import jax.numpy as jnp
from jax import lax
from jax.experimental import pallas as pl
from jax.experimental.pallas import tpu as pltpu
from jax.sharding import PartitionSpec as P

MESH = pl.DeviceIdType.MESH
BLK = 128
MOST = 4
HALF = MOST // 2
META = 16
ROWS = HALF * BLK + META
BARRIER_AT = 4
AHEAD = 2
TURNS = (
    ((1, 0), (-1, 0), (0, 1), (0, -1), (2, 2)),
    ((1, 1), (-1, -1), (1, -1), (-1, 1)),
    ((2, 0), (1, 2), (-1, 2)),
    ((0, 2), (2, 1), (2, -1)),
)
WIDTH = max(len(turns) for turns in TURNS)


def sign_table(rows, cols):
    shared = lax.broadcasted_iota(jnp.int32, (rows, cols), 0) & (
        lax.broadcasted_iota(jnp.int32, (rows, cols), 1) & (BLK - 1)
    )
    shared = shared ^ (shared >> 4)
    shared = shared ^ (shared >> 2)
    shared = shared ^ (shared >> 1)
    return (1 - 2 * (shared & 1)).astype(jnp.float32).astype(jnp.bfloat16)


def push_kernel(
    sizes, trained, snapshot, changed_in, placement_in, result, new_bufs, old_bufs, changed, placement, table, mine, other, staged, passing, sems
):
    expert_count, tensor_count, local_experts, block_rows = sizes
    (in_sem, table_sem, swap_send, swap_recv, plane_send, plane_recv, z_send, z_recv, last_send, last_recv) = sems
    c = lax.axis_index("expert")
    z = lax.axis_index("tensor")
    r = lax.axis_index("replica")
    slots = expert_count
    group = expert_count // tensor_count
    side = math.isqrt(expert_count)

    small_loads = (
        pltpu.make_async_copy(changed_in, changed, table_sem.at[0]),
        pltpu.make_async_copy(placement_in, placement, table_sem.at[1]),
    )
    loads = [
        (
            pltpu.make_async_copy(trained.at[e], new_bufs[e], in_sem.at[0, e]),
            pltpu.make_async_copy(snapshot.at[e], old_bufs[e], in_sem.at[1, e]),
        )
        for e in range(local_experts)
    ]
    for load in small_loads:
        load.start()
    for pair in loads:
        for load in pair:
            load.start()

    barrier = pltpu.get_barrier_semaphore()

    pl.semaphore_signal(barrier, inc=1, device_id=(c, z, 1 - r), device_id_type=MESH)

    @pl.loop(1, expert_count)
    def _(step):
        pl.semaphore_signal(barrier, inc=1, device_id=(lax.rem(c + step, expert_count), z, r), device_id_type=MESH)

    @pl.loop(1, tensor_count)
    def _(step):
        pl.semaphore_signal(barrier, inc=1, device_id=(c, lax.rem(z + step, tensor_count), r), device_id_type=MESH)

    table[...] = sign_table(BLK, 2 * BLK)
    for load in small_loads:
        load.wait()

    def remote(src, dst, send_sem, recv_sem, device):
        return pltpu.make_async_remote_copy(
            src_ref=src, dst_ref=dst, send_sem=send_sem, recv_sem=recv_sem, device_id=device, device_id_type=MESH
        )

    def swap(e):
        return remote(other.at[e], mine.at[r * local_experts + e], swap_send.at[e], swap_recv.at[e], (c, z, 1 - r))

    row_ids = lax.broadcasted_iota(jnp.int32, (META, BLK), 0)

    for e in range(local_experts):
        count = jnp.int32(0)
        spots = [jnp.int32(block_rows)] * MOST
        picks = [jnp.int32(0)] * MOST
        for b in range(block_rows):
            flag = changed[b, 0, e]
            for k in range(MOST):
                hit = (flag == 1) & (count == k)
                spots[k] = jnp.where(hit, b, spots[k])
                picks[k] = jnp.where(hit, b, picks[k])
            count = count + flag
        for load in loads[e]:
            load.wait()
        highs, lows = [], []
        for k in range(MOST):
            delta = new_bufs[e][picks[k]] - old_bufs[e][picks[k]].astype(jnp.float32)
            high = delta.astype(jnp.bfloat16)
            highs.append(high)
            lows.append((delta - high.astype(jnp.float32)).astype(jnp.bfloat16))
        parts = jnp.concatenate([jnp.concatenate(highs, axis=1), jnp.concatenate(lows, axis=1)], axis=0)
        coded = jnp.dot(table[...], parts, preferred_element_type=jnp.float32) * (1.0 / math.sqrt(BLK))
        coded = coded.astype(jnp.bfloat16)

        def store(ref, index, first, coded=coded, spots=spots):
            for k in range(HALF):
                ref[index, k * BLK : (k + 1) * BLK, :] = coded[:, (first + k) * BLK : (first + k + 1) * BLK]
            spot = jnp.where(row_ids < META // 2, spots[first], spots[first + 1])
            ref[index, HALF * BLK : ROWS, :] = spot.astype(jnp.float32).astype(jnp.bfloat16)

        own = r * local_experts + e

        @pl.when(r == 0)
        def _():
            store(mine, own, 0)
            store(other, e, HALF)

        @pl.when(r == 1)
        def _():
            store(mine, own, HALF)
            store(other, e, 0)

        if e == BARRIER_AT:
            pl.semaphore_wait(barrier, expert_count + tensor_count - 1)
            for before in range(e):
                swap(before).start()
        elif e > BARRIER_AT:
            swap(e - 1).start()

    swap(local_experts - 1).start()

    @pl.loop(0, local_experts)
    def _(e):
        swap(e).wait_recv()

    home = c // group == z
    spot_here = z * group + lax.rem(c, group)

    def along(source):
        spot = z * group + lax.rem(source, group)
        return remote(
            passing.at[source], result.at[r, spot], z_send.at[source], z_recv.at[spot], (c, source // group, r)
        )

    @pl.when(home)
    def _():
        result[r, c] = mine[placement[c]]

    @pl.when(jnp.logical_not(home))
    def _():
        passing[c] = mine[placement[c]]

    def plane(s):
        return remote(staged.at[s], passing.at[c], plane_send.at[s], plane_recv.at[c], (s, z, r))

    def plane_home(s):
        return remote(staged.at[s], result.at[r, spot_here], plane_send.at[s], z_recv.at[spot_here], (s, z, r))

    def plane_from(source):
        return remote(staged.at[source], passing.at[source], plane_send.at[source], plane_recv.at[source], (source, z, r))

    def shifted(dx, dy):
        return lax.rem(c // side + dx + side, side) * side + lax.rem(lax.rem(c, side) + dy + side, side)

    def group_turns(place):
        which = lax.rem(place + z + 2 * r, len(TURNS))
        steps = []
        for axis in range(2):
            packed = [sum((turn[axis] % side) << (4 * k) for k, turn in enumerate(turns)) for turns in TURNS]
            code = jnp.int32(packed[0])
            for g in range(1, len(TURNS)):
                code = jnp.where(which == g, packed[g], code)
            steps.append([(code >> (4 * k)) & (side - 1) for k in range(WIDTH)])
        return tuple(zip(*steps))

    def issue(turns):
        targets = [shifted(dx, dy) for dx, dy in turns]
        for s in targets:
            staged[s] = mine[placement[s]]
        for s in targets:

            @pl.when((s != c) & home)
            def _():
                plane_home(s).start()

            @pl.when((s != c) & jnp.logical_not(home))
            def _():
                plane(s).start()

    def forward(turns):
        for dx, dy in turns:
            source = shifted(side - dx, side - dy)

            @pl.when((source != c) & (source // group != z))
            def _():
                plane_from(source).wait_recv()
                along(source).start()

    @pl.when(jnp.logical_not(home))
    def _():
        along(c).start()

    order = [group_turns(place) for place in range(len(TURNS))]
    for turns in order[:AHEAD]:
        issue(turns)
    for g, turns in enumerate(order):
        forward(turns)
        if g + AHEAD < len(order):
            issue(order[g + AHEAD])

    @pl.loop(0, local_experts)
    def _(e):
        swap(e).wait_send()

    @pl.loop(0, slots)
    def _(s):
        @pl.when(s != c)
        def _():
            plane(s).wait_send()

    def last(spot):
        return remote(
            result.at[r, spot], result.at[r, spot], last_send.at[spot], last_recv.at[spot], (c, z, 1 - r)
        )

    def arrived(spot):
        return remote(result.at[r, spot], result.at[r, spot], z_send.at[spot], z_recv.at[spot], (c, z, 1 - r))

    def last_from(spot):
        return remote(result.at[1 - r, spot], result.at[1 - r, spot], last_send.at[spot], last_recv.at[spot], (c, z, 1 - r))

    @pl.loop(0, slots)
    def _(step):
        far = (step // group + 1) // 2
        away = jnp.where(lax.rem(step // group, 2) == 1, far, tensor_count - far)
        spot = lax.rem(z + away, tensor_count) * group + lax.rem(step, group)

        @pl.when(jnp.logical_not(home & (spot == c)))
        def _():
            arrived(spot).wait_recv()

        last(spot).start()

    @pl.loop(0, slots)
    def _(s):
        @pl.when(s // group != z)
        def _():
            along(s).wait_send()

        last(s).wait_send()

    @pl.loop(0, slots)
    def _(s):
        last_from(s).wait_recv()


def push(trained, snapshot, changed, placement):
    block_rows, _, local_experts = changed.shape
    slots = placement.shape[0]
    sizes = (lax.axis_size("expert"), lax.axis_size("tensor"), local_experts, block_rows)
    dma = pltpu.SemaphoreType.DMA

    def kernel(a, b, c, d, result, *refs):
        new_bufs, old_bufs, refs = refs[:local_experts], refs[local_experts : 2 * local_experts], refs[2 * local_experts :]
        push_kernel(sizes, a, b, c, d, result, new_bufs, old_bufs, *refs[:7], refs[7:])

    return pl.pallas_call(
        kernel,
        name="push",
        out_shape=pltpu.VMEM((2, slots, ROWS, BLK), jnp.bfloat16),
        in_specs=[
            pl.BlockSpec(memory_space=pltpu.HBM),
            pl.BlockSpec(memory_space=pltpu.HBM),
            pl.BlockSpec(memory_space=pltpu.HBM),
            pl.BlockSpec(memory_space=pltpu.HBM),
        ],
        out_specs=pl.BlockSpec(memory_space=pltpu.VMEM),
        scratch_shapes=[
            *[pltpu.VMEM(trained.shape[1:], jnp.float32) for _ in range(local_experts)],
            *[pltpu.VMEM(snapshot.shape[1:], jnp.bfloat16) for _ in range(local_experts)],
            pltpu.SMEM(changed.shape, jnp.int32),
            pltpu.SMEM(placement.shape, jnp.int32),
            pltpu.VMEM((BLK, 2 * BLK), jnp.bfloat16),
            pltpu.VMEM((slots, ROWS, BLK), jnp.bfloat16),
            pltpu.VMEM((local_experts, ROWS, BLK), jnp.bfloat16),
            pltpu.VMEM((slots, ROWS, BLK), jnp.bfloat16),
            pltpu.VMEM((slots, ROWS, BLK), jnp.bfloat16),
            dma((2, local_experts)),
            dma((2,)),
            dma((local_experts,)),
            dma((local_experts,)),
            dma((slots,)),
            dma((slots,)),
            dma((slots,)),
            dma((slots,)),
            dma((slots,)),
            dma((slots,)),
        ],
        compiler_params=pltpu.CompilerParams(collective_id=0, has_side_effects=True, vmem_limit_bytes=60 * 1024 * 1024),
    )(trained, snapshot, changed, placement)


def spread_kernel(sizes, tiles, out, image, sems):
    tensor_count, group, block_rows = sizes

    def write(z):
        rows = pl.ds(pl.multiple_of(z * block_rows * BLK, BLK), block_rows * BLK)
        return pltpu.make_async_copy(image.at[z], out.at[0, rows, :], sems.at[z])

    @pl.loop(0, tensor_count)
    def _(z):
        for j in range(group):
            index = z * group + j
            spots = []
            for k in range(MOST):
                row = HALF * BLK + (k % HALF) * (META // HALF)
                spots.append(tiles[k // HALF, index, row : row + 1, :])
            chunk = 32
            for b in range(block_rows):
                masks = [jnp.broadcast_to(spots[k] == jnp.bfloat16(b), (chunk, BLK)) for k in range(MOST)]
                for first in range(0, BLK, chunk):
                    value = jnp.zeros((chunk, BLK), jnp.bfloat16)
                    for k in range(MOST):
                        row = (k % HALF) * BLK + first
                        value = jnp.where(masks[k], tiles[k // HALF, index, row : row + chunk, :], value)
                    image[z, b * BLK + first : b * BLK + first + chunk, j * BLK : (j + 1) * BLK] = value
        write(z).start()

    @pl.loop(0, tensor_count)
    def _(z):
        write(z).wait()


def spread(tiles, block_rows):
    tensor_count = lax.axis_size("tensor")
    group = tiles.shape[1] // tensor_count
    rows = block_rows * BLK

    def kernel(tiles_ref, out, image, sems):
        spread_kernel((tensor_count, group, block_rows), tiles_ref, out, image, sems)

    return pl.pallas_call(
        kernel,
        name="spread",
        out_shape=jax.ShapeDtypeStruct((1, tensor_count * rows, group * BLK), jnp.bfloat16),
        in_specs=[pl.BlockSpec(memory_space=pltpu.VMEM)],
        out_specs=pl.BlockSpec(memory_space=pl.ANY),
        scratch_shapes=[
            pltpu.VMEM((tensor_count, rows, group * BLK), jnp.bfloat16),
            pltpu.SemaphoreType.DMA((tensor_count,)),
        ],
        compiler_params=pltpu.CompilerParams(vmem_limit_bytes=24 * 1024 * 1024),
    )(tiles)


def body(trained, snapshot, changed, placement):
    local_experts, local_rows, _ = trained.shape
    block_rows = local_rows // BLK
    blocks = (local_experts, block_rows, BLK, BLK)
    tiles = push(trained.reshape(blocks), snapshot.reshape(blocks), changed.transpose(1, 2, 0), placement)
    return spread(tiles, block_rows)


def solution(mesh):
    in_specs = (
        P("replica", "tensor", "expert"),
        P("replica", "tensor", "expert"),
        P("replica", "tensor", "expert"),
        P(),
    )
    out_specs = P("expert", None, "tensor")
    return jax.shard_map(body, mesh=mesh, in_specs=in_specs, out_specs=out_specs, check_vma=False)
```

time: 58.9 us -> 49 us (0.83)
  the two profiles are of different devices: /device:TPU:1 before, /device:TPU:33 now
where the time goes in v2:
time: 49 us; the launch traced here: 48.9 us
  Pallas kernels  48.9 us (100%)
    pallas_call x1, Pallas kernels, push(): pl.pallas_call(kernel, name='push', out_shape=pltpu.VMEM((2, slots, ROWS,...  46.3 us
    pallas_call x1, Pallas kernels, spread(): pl.pallas_call(kernel, name='spread', out_shape=jax.ShapeDtypeStruct((1,...  2.62 us

profile of v2, /device:TPU:33, one launch (start us, length us, event | category | flops | bytes accessed | tf_op | source)
XLA Modules:
  0.0 48.9 jit_solution(7675444870389472769)
XLA Ops:
  0.0 46.3 %push.1.tiles_ref = bf16[2,16,272,128]{3,2,1,0:T(8,128)(2,1)S(1)} custom-call(f32[8,7,128,128]{3,2,1,0:T(8,128)} %bitcast.3, bf16[8,7,128,128]{3,2,1,0:T(8,128)(2,1)} %bitcast.4, s32[7,1,8]{2,1,0:T(1,128)} %bitcast.5, s32[16]{0:T(128)} %d.1), custom_call_target="tpu_custom_call" | custom-call | tf_op jit(solution)/shard_map/push/pallas_call | solution.py:277
  46.3 2.6 %spread.1 = bf16[1,7168,256]{2,1,0:T(8,128)(2,1)} custom-call(bf16[2,16,272,128]{3,2,1,0:T(8,128)(2,1)S(1)} %push.1.tiles_ref), custom_call_target="tpu_custom_call" | custom-call | tf_op jit(solution)/shard_map/spread/pallas_call | solution.py:352

commit v3 on v2

--- a/solution.py
+++ b/solution.py
@@ -11,17 +11,20 @@
 BLK = 128
 MOST = 4
 HALF = MOST // 2
-META = 16
+META = 8
 ROWS = HALF * BLK + META
 BARRIER_AT = 4
-AHEAD = 2
+WINDOW = 10
+RAMP = 10
+CHUNK = 64
+TOGETHER = 2
+PIECES = ((0, BLK), (BLK, ROWS - BLK))
 TURNS = (
-    ((1, 0), (-1, 0), (0, 1), (0, -1), (2, 2)),
-    ((1, 1), (-1, -1), (1, -1), (-1, 1)),
-    ((2, 0), (1, 2), (-1, 2)),
-    ((0, 2), (2, 1), (2, -1)),
+    ((1, 0), (-1, 0), (0, 1), (0, -1)),
+    ((1, 1), (-1, -1), (2, 0), (0, 2)),
+    ((1, -1), (-1, 1), (2, 2), (0, 0)),
+    ((2, 1), (2, -1), (1, 2), (-1, 2)),
 )
-WIDTH = max(len(turns) for turns in TURNS)
 
 
 def sign_table(rows, cols):
@@ -85,11 +88,11 @@
         )
 
     def swap(e):
-        return remote(other.at[e], mine.at[r * local_experts + e], swap_send.at[e], swap_recv.at[e], (c, z, 1 - r))
+        return remote(other.at[e], mine.at[r * local_experts + e], swap_send, swap_recv, (c, z, 1 - r))
 
     row_ids = lax.broadcasted_iota(jnp.int32, (META, BLK), 0)
 
-    for e in range(local_experts):
+    def chosen(e):
         count = jnp.int32(0)
         spots = [jnp.int32(block_rows)] * MOST
         picks = [jnp.int32(0)] * MOST
@@ -100,56 +103,63 @@
                 spots[k] = jnp.where(hit, b, spots[k])
                 picks[k] = jnp.where(hit, b, picks[k])
             count = count + flag
-        for load in loads[e]:
-            load.wait()
+        return spots, picks
+
+    for start in range(0, local_experts, TOGETHER):
+        batch = range(start, start + TOGETHER)
+        places = [chosen(e) for e in batch]
+        for e in batch:
+            for load in loads[e]:
+                load.wait()
         highs, lows = [], []
-        for k in range(MOST):
-            delta = new_bufs[e][picks[k]] - old_bufs[e][picks[k]].astype(jnp.float32)
-            high = delta.astype(jnp.bfloat16)
-            highs.append(high)
-            lows.append((delta - high.astype(jnp.float32)).astype(jnp.bfloat16))
+        for e, (_, picks) in zip(batch, places):
+            for pick in picks:
+                delta = new_bufs[e][pick] - old_bufs[e][pick].astype(jnp.float32)
+                high = delta.astype(jnp.bfloat16)
+                highs.append(high)
+                lows.append((delta - high.astype(jnp.float32)).astype(jnp.bfloat16))
         parts = jnp.concatenate([jnp.concatenate(highs, axis=1), jnp.concatenate(lows, axis=1)], axis=0)
         coded = jnp.dot(table[...], parts, preferred_element_type=jnp.float32) * (1.0 / math.sqrt(BLK))
         coded = coded.astype(jnp.bfloat16)
 
-        def store(ref, index, first, coded=coded, spots=spots):
+        def store(ref, index, i, first, coded=coded, places=places):
             for k in range(HALF):
-                ref[index, k * BLK : (k + 1) * BLK, :] = coded[:, (first + k) * BLK : (first + k + 1) * BLK]
+                column = (i * MOST + first + k) * BLK
+                ref[index, k * BLK : (k + 1) * BLK, :] = coded[:, column : column + BLK]
+            spots = places[i][0]
             spot = jnp.where(row_ids < META // 2, spots[first], spots[first + 1])
             ref[index, HALF * BLK : ROWS, :] = spot.astype(jnp.float32).astype(jnp.bfloat16)
 
-        own = r * local_experts + e
-
-        @pl.when(r == 0)
-        def _():
-            store(mine, own, 0)
-            store(other, e, HALF)
-
-        @pl.when(r == 1)
-        def _():
-            store(mine, own, HALF)
-            store(other, e, 0)
-
-        if e == BARRIER_AT:
+        for low in range(2):
+
+            @pl.when(r == low)
+            def _(low=low):
+                for i, e in enumerate(batch):
+                    store(mine, r * local_experts + e, i, low * HALF)
+                    store(other, e, i, (1 - low) * HALF)
+
+        if start == BARRIER_AT:
             pl.semaphore_wait(barrier, expert_count + tensor_count - 1)
-            for before in range(e):
-                swap(before).start()
-        elif e > BARRIER_AT:
-            swap(e - 1).start()
-
-    swap(local_experts - 1).start()
-
-    @pl.loop(0, local_experts)
-    def _(e):
-        swap(e).wait_recv()
+            for e in range(start):
+                swap(e).start()
+        elif start > BARRIER_AT:
+            for e in range(start - TOGETHER, start):
+                swap(e).start()
+
+    for e in range(local_experts - TOGETHER, local_experts):
+        swap(e).start()
+
+    arrivals = mine.at[pl.ds((1 - r) * local_experts, local_experts)]
+    pltpu.make_async_copy(arrivals, arrivals, swap_recv).wait()
 
     home = c // group == z
     spot_here = z * group + lax.rem(c, group)
 
-    def along(source):
+    def along(source, piece):
         spot = z * group + lax.rem(source, group)
+        rows = pl.ds(*PIECES[piece])
         return remote(
-            passing.at[source], result.at[r, spot], z_send.at[source], z_recv.at[spot], (c, source // group, r)
+            passing.at[source, rows], result.at[r, spot, rows], z_send, z_recv.at[spot], (c, source // group, r)
         )
 
     @pl.when(home)
@@ -160,14 +170,19 @@
     def _():
         passing[c] = mine[placement[c]]
 
-    def plane(s):
-        return remote(staged.at[s], passing.at[c], plane_send.at[s], plane_recv.at[c], (s, z, r))
-
-    def plane_home(s):
-        return remote(staged.at[s], result.at[r, spot_here], plane_send.at[s], z_recv.at[spot_here], (s, z, r))
-
-    def plane_from(source):
-        return remote(staged.at[source], passing.at[source], plane_send.at[source], plane_recv.at[source], (source, z, r))
+    def plane(s, piece):
+        rows = pl.ds(*PIECES[piece])
+        return remote(staged.at[s, rows], passing.at[c, rows], plane_send, plane_recv.at[piece, c], (s, z, r))
+
+    def plane_home(s, piece):
+        rows = pl.ds(*PIECES[piece])
+        return remote(staged.at[s, rows], result.at[r, spot_here, rows], plane_send, z_recv.at[spot_here], (s, z, r))
+
+    def plane_from(source, piece):
+        rows = pl.ds(*PIECES[piece])
+        return remote(
+            staged.at[source, rows], passing.at[source, rows], plane_send, plane_recv.at[piece, source], (source, z, r)
+        )
 
     def shifted(dx, dy):
         return lax.rem(c // side + dx + side, side) * side + lax.rem(lax.rem(c, side) + dy + side, side)
@@ -180,64 +195,68 @@
             code = jnp.int32(packed[0])
             for g in range(1, len(TURNS)):
                 code = jnp.where(which == g, packed[g], code)
-            steps.append([(code >> (4 * k)) & (side - 1) for k in range(WIDTH)])
-        return tuple(zip(*steps))
-
-    def issue(turns):
-        targets = [shifted(dx, dy) for dx, dy in turns]
-        for s in targets:
-            staged[s] = mine[placement[s]]
-        for s in targets:
-
-            @pl.when((s != c) & home)
-            def _():
-                plane_home(s).start()
-
-            @pl.when((s != c) & jnp.logical_not(home))
-            def _():
-                plane(s).start()
-
-    def forward(turns):
-        for dx, dy in turns:
-            source = shifted(side - dx, side - dy)
-
-            @pl.when((source != c) & (source // group != z))
-            def _():
-                plane_from(source).wait_recv()
-                along(source).start()
+            steps.append([(code >> (4 * k)) & (side - 1) for k in range(len(TURNS[0]))])
+        return list(zip(*steps))
+
+    def stage(turn):
+        s = shifted(*turn)
+        staged[s] = mine[placement[s]]
+
+    def issue(turn, piece):
+        s = shifted(*turn)
+
+        @pl.when((s != c) & home)
+        def _():
+            plane_home(s, piece).start()
+
+        @pl.when((s != c) & jnp.logical_not(home))
+        def _():
+            plane(s, piece).start()
+
+    def forward(turn, piece):
+        source = shifted(side - turn[0], side - turn[1])
+
+        @pl.when((source != c) & (source // group != z))
+        def _():
+            plane_from(source, piece).wait_recv()
+            along(source, piece).start()
+
+    order = sum([group_turns(place) for place in range(len(TURNS))], [])
+    pieces = [(turn, piece) for turn in order for piece in range(len(PIECES))]
+    early = -(-RAMP // len(PIECES))
+    for turn in order[:early]:
+        stage(turn)
+    for item in pieces[:RAMP]:
+        issue(*item)
 
     @pl.when(jnp.logical_not(home))
     def _():
-        along(c).start()
-
-    order = [group_turns(place) for place in range(len(TURNS))]
-    for turns in order[:AHEAD]:
-        issue(turns)
-    for g, turns in enumerate(order):
-        forward(turns)
-        if g + AHEAD < len(order):
-            issue(order[g + AHEAD])
-
-    @pl.loop(0, local_experts)
-    def _(e):
-        swap(e).wait_send()
-
-    @pl.loop(0, slots)
-    def _(s):
-        @pl.when(s != c)
-        def _():
-            plane(s).wait_send()
+        for piece in range(len(PIECES)):
+            along(c, piece).start()
+
+    for turn in order[early:]:
+        stage(turn)
+    issued = RAMP
+    for i, item in enumerate(pieces):
+        forward(*item)
+        upto = min(i + 1 + min(RAMP + i + 1, WINDOW), len(pieces))
+        for later in pieces[issued:upto]:
+            issue(*later)
+        issued = max(issued, upto)
+
+    def settle(ref, sem):
+        pltpu.make_async_copy(ref, ref, sem).wait()
+
+    settle(other, swap_send)
+    settle(staged.at[pl.ds(0, slots - 1)], plane_send)
 
     def last(spot):
         return remote(
-            result.at[r, spot], result.at[r, spot], last_send.at[spot], last_recv.at[spot], (c, z, 1 - r)
+            result.at[r, spot], result.at[r, spot], last_send, last_recv, (c, z, 1 - r)
         )
 
     def arrived(spot):
-        return remote(result.at[r, spot], result.at[r, spot], z_send.at[spot], z_recv.at[spot], (c, z, 1 - r))
-
-    def last_from(spot):
-        return remote(result.at[1 - r, spot], result.at[1 - r, spot], last_send.at[spot], last_recv.at[spot], (c, z, 1 - r))
+        return remote(result.at[r, spot], result.at[r, spot], z_send, z_recv.at[spot], (c, z, 1 - r))
 
     @pl.loop(0, slots)
     def _(step):
@@ -251,17 +270,9 @@
 
         last(spot).start()
 
-    @pl.loop(0, slots)
-    def _(s):
-        @pl.when(s // group != z)
-        def _():
-            along(s).wait_send()
-
-        last(s).wait_send()
-
-    @pl.loop(0, slots)
-    def _(s):
-        last_from(s).wait_recv()
+    settle(passing.at[pl.ds(0, slots - group)], z_send)
+    settle(result.at[r], last_send)
+    settle(result.at[1 - r], last_recv)
 
 
 def push(trained, snapshot, changed, placement):
@@ -297,14 +308,14 @@
             pltpu.VMEM((slots, ROWS, BLK), jnp.bfloat16),
             dma((2, local_experts)),
             dma((2,)),
-            dma((local_experts,)),
-            dma((local_experts,)),
+            dma,
+            dma,
+            dma,
+            dma((len(PIECES), slots)),
+            dma,
             dma((slots,)),
-            dma((slots,)),
-            dma((slots,)),
-            dma((slots,)),
-            dma((slots,)),
-            dma((slots,)),
+            dma,
+            dma,
         ],
         compiler_params=pltpu.CompilerParams(collective_id=0, has_side_effects=True, vmem_limit_bytes=60 * 1024 * 1024),
     )(trained, snapshot, changed, placement)
@@ -324,16 +335,17 @@
             spots = []
             for k in range(MOST):
                 row = HALF * BLK + (k % HALF) * (META // HALF)
-                spots.append(tiles[k // HALF, index, row : row + 1, :])
-            chunk = 32
-            for b in range(block_rows):
-                masks = [jnp.broadcast_to(spots[k] == jnp.bfloat16(b), (chunk, BLK)) for k in range(MOST)]
-                for first in range(0, BLK, chunk):
-                    value = jnp.zeros((chunk, BLK), jnp.bfloat16)
+                spots.append(jnp.broadcast_to(tiles[k // HALF, index, row : row + 1, :], (CHUNK, BLK)))
+            for first in range(0, BLK, CHUNK):
+                values = []
+                for k in range(MOST):
+                    row = (k % HALF) * BLK + first
+                    values.append(tiles[k // HALF, index, row : row + CHUNK, :])
+                for b in range(block_rows):
+                    value = jnp.zeros((CHUNK, BLK), jnp.bfloat16)
                     for k in range(MOST):
-                        row = (k % HALF) * BLK + first
-                        value = jnp.where(masks[k], tiles[k // HALF, index, row : row + chunk, :], value)
-                    image[z, b * BLK + first : b * BLK + first + chunk, j * BLK : (j + 1) * BLK] = value
+                        value = jnp.where(spots[k] == jnp.bfloat16(b), values[k], value)
+                    image[z, b * BLK + first : b * BLK + first + CHUNK, j * BLK : (j + 1) * BLK] = value
         write(z).start()
 
     @pl.loop(0, tensor_count)

time: 49 us -> 45.9 us (0.937)
  Pallas kernels: 48.9 us -> 45.8 us
    pallas_call x1, Pallas kernels: 46.3 us -> 43.8 us  [push(): pl.pallas_call(kernel, name='push', out_shape=pltpu.VMEM((2, slots, ROWS,...]
    pallas_call x1, Pallas kernels: 2.62 us -> 2.01 us  [spread(): pl.pallas_call(kernel, name='spread', out_shape=jax.ShapeDtypeStruct((1,...]
where the time goes in v3:
time: 45.9 us; the launch traced here: 45.8 us
  Pallas kernels  45.8 us (100%)
    pallas_call x1, Pallas kernels, push(): pl.pallas_call(kernel, name='push', out_shape=pltpu.VMEM((2, slots, ROWS,...  43.8 us
    pallas_call x1, Pallas kernels, spread(): pl.pallas_call(kernel, name='spread', out_shape=jax.ShapeDtypeStruct((1,...  2.01 us

profile of v3, /device:TPU:33, one launch (start us, length us, event | category | flops | bytes accessed | tf_op | source)
XLA Modules:
  0.0 45.8 jit_solution(16119741207419072198)
XLA Ops:
  0.0 43.8 %push.1.tiles_ref = bf16[2,16,264,128]{3,2,1,0:T(8,128)(2,1)S(1)} custom-call(f32[8,7,128,128]{3,2,1,0:T(8,128)} %bitcast.3, bf16[8,7,128,128]{3,2,1,0:T(8,128)(2,1)} %bitcast.4, s32[7,1,8]{2,1,0:T(1,128)} %bitcast.5, s32[16]{0:T(128)} %d.1), custom_call_target="tpu_custom_call" | custom-call | tf_op jit(solution)/shard_map/push/pallas_call | solution.py:288
  43.8 2.0 %spread.1 = bf16[1,7168,256]{2,1,0:T(8,128)(2,1)} custom-call(bf16[2,16,264,128]{3,2,1,0:T(8,128)(2,1)S(1)} %push.1.tiles_ref), custom_call_target="tpu_custom_call" | custom-call | tf_op jit(solution)/shard_map/spread/pallas_call | solution.py:364

commit v4 on v3

--- a/solution.py
+++ b/solution.py
@@ -20,8 +20,8 @@
 TOGETHER = 2
 PIECES = ((0, BLK), (BLK, ROWS - BLK))
 TURNS = (
-    ((1, 0), (-1, 0), (0, 1), (0, -1)),
-    ((1, 1), (-1, -1), (2, 0), (0, 2)),
+    ((0, 1), (0, -1), (1, 0), (-1, 0)),
+    ((2, 0), (0, 2), (1, 1), (-1, -1)),
     ((1, -1), (-1, 1), (2, 2), (0, 0)),
     ((2, 1), (2, -1), (1, 2), (-1, 2)),
 )
@@ -60,23 +60,19 @@
         )
         for e in range(local_experts)
     ]
-    for load in small_loads:
+    for load in (*small_loads, *loads[0]):
         load.start()
-    for pair in loads:
+
+    barrier = pltpu.get_barrier_semaphore()
+    for step in range(1, tensor_count):
+        pl.semaphore_signal(barrier, inc=1, device_id=(c, lax.rem(z + step, tensor_count), r), device_id_type=MESH)
+    for step in range(1, expert_count):
+        pl.semaphore_signal(barrier, inc=1, device_id=(lax.rem(c + step, expert_count), z, r), device_id_type=MESH)
+    pl.semaphore_signal(barrier, inc=1, device_id=(c, z, 1 - r), device_id_type=MESH)
+
+    for pair in loads[1:]:
         for load in pair:
             load.start()
-
-    barrier = pltpu.get_barrier_semaphore()
-
-    pl.semaphore_signal(barrier, inc=1, device_id=(c, z, 1 - r), device_id_type=MESH)
-
-    @pl.loop(1, expert_count)
-    def _(step):
-        pl.semaphore_signal(barrier, inc=1, device_id=(lax.rem(c + step, expert_count), z, r), device_id_type=MESH)
-
-    @pl.loop(1, tensor_count)
-    def _(step):
-        pl.semaphore_signal(barrier, inc=1, device_id=(c, lax.rem(z + step, tensor_count), r), device_id_type=MESH)
 
     table[...] = sign_table(BLK, 2 * BLK)
     for load in small_loads:

time: 45.9 us -> 45.3 us (0.987)
  Pallas kernels: 45.8 us -> 45.2 us
    pallas_call x1, Pallas kernels: 43.8 us -> 43.2 us  [push(): pl.pallas_call(kernel, name='push', out_shape=pltpu.VMEM((2, slots, ROWS,...]
where the time goes in v4:
time: 45.3 us; the launch traced here: 45.2 us
  Pallas kernels  45.2 us (100%)
    pallas_call x1, Pallas kernels, push(): pl.pallas_call(kernel, name='push', out_shape=pltpu.VMEM((2, slots, ROWS,...  43.2 us
    pallas_call x1, Pallas kernels, spread(): pl.pallas_call(kernel, name='spread', out_shape=jax.ShapeDtypeStruct((1,...  2.01 us

profile of v4, /device:TPU:33, one launch (start us, length us, event | category | flops | bytes accessed | tf_op | source)
XLA Modules:
  0.0 45.2 jit_solution(1004896937081668114)
XLA Ops:
  0.0 43.2 %push.1.tiles_ref = bf16[2,16,264,128]{3,2,1,0:T(8,128)(2,1)S(1)} custom-call(f32[8,7,128,128]{3,2,1,0:T(8,128)} %bitcast.3, bf16[8,7,128,128]{3,2,1,0:T(8,128)(2,1)} %bitcast.4, s32[7,1,8]{2,1,0:T(1,128)} %bitcast.5, s32[16]{0:T(128)} %d.1), custom_call_target="tpu_custom_call" | custom-call | tf_op jit(solution)/shard_map/push/pallas_call | solution.py:284
  43.2 2.0 %spread.1 = bf16[1,7168,256]{2,1,0:T(8,128)(2,1)} custom-call(bf16[2,16,264,128]{3,2,1,0:T(8,128)(2,1)S(1)} %push.1.tiles_ref), custom_call_target="tpu_custom_call" | custom-call | tf_op jit(solution)/shard_map/spread/pallas_call | solution.py:360

commit v5 on v4

--- a/solution.py
+++ b/solution.py
@@ -218,17 +218,17 @@
             along(source, piece).start()
 
     order = sum([group_turns(place) for place in range(len(TURNS))], [])
+    @pl.when(jnp.logical_not(home))
+    def _():
+        for piece in range(len(PIECES)):
+            along(c, piece).start()
+
     pieces = [(turn, piece) for turn in order for piece in range(len(PIECES))]
     early = -(-RAMP // len(PIECES))
     for turn in order[:early]:
         stage(turn)
     for item in pieces[:RAMP]:
         issue(*item)
-
-    @pl.when(jnp.logical_not(home))
-    def _():
-        for piece in range(len(PIECES)):
-            along(c, piece).start()
 
     for turn in order[early:]:
         stage(turn)

time: 45.3 us -> 45.3 us (level)
  no operation moved by 1% of the time
where the time goes in v5:
time: 45.3 us; the launch traced here: 45.2 us
  Pallas kernels  45.2 us (100%)
    pallas_call x1, Pallas kernels, push(): pl.pallas_call(kernel, name='push', out_shape=pltpu.VMEM((2, slots, ROWS,...  43.2 us
    pallas_call x1, Pallas kernels, spread(): pl.pallas_call(kernel, name='spread', out_shape=jax.ShapeDtypeStruct((1,...  2.01 us

profile of v5, /device:TPU:33, one launch (start us, length us, event | category | flops | bytes accessed | tf_op | source)
XLA Modules:
  0.0 45.2 jit_solution(4628275838298202186)
XLA Ops:
  0.0 43.2 %push.1.tiles_ref = bf16[2,16,264,128]{3,2,1,0:T(8,128)(2,1)S(1)} custom-call(f32[8,7,128,128]{3,2,1,0:T(8,128)} %bitcast.3, bf16[8,7,128,128]{3,2,1,0:T(8,128)(2,1)} %bitcast.4, s32[7,1,8]{2,1,0:T(1,128)} %bitcast.5, s32[16]{0:T(128)} %d.1), custom_call_target="tpu_custom_call" | custom-call | tf_op jit(solution)/shard_map/push/pallas_call | solution.py:284
  43.2 2.0 %spread.1 = bf16[1,7168,256]{2,1,0:T(8,128)(2,1)} custom-call(bf16[2,16,264,128]{3,2,1,0:T(8,128)(2,1)S(1)} %push.1.tiles_ref), custom_call_target="tpu_custom_call" | custom-call | tf_op jit(solution)/shard_map/spread/pallas_call | solution.py:360
